TPU v7x, 32 devices: a whole 2x2x4 slice. The times are simulated.
32 devices in a mesh: rep: 4 (over z), tp: 8 (over y, x, core).
Axes of the slice: x: 2, y: 2, z: 4, core: 2. Of those that a mesh axis runs over, the one named last changes fastest.
Arguments:
- attn: bfloat16 [3072, 4096], P('rep', 'tp'), parts along dimension 0, may hold values from -6 to 6
- output_weight: bfloat16 [4096, 8192], P(None, 'tp'), may hold values from -0.09375 to 0.09375
- adapter_down_weight: bfloat16 [8, 64, 4096], P('tp'), may hold values from -0.09375 to 0.09375
- adapter_up_weight: bfloat16 [8, 64, 8192], P('tp'), may hold values from -0.75 to 0.75
- block_adapter_index: int32 [24], P('rep'), parts along dimension 0, may hold values from 0 to 7
- adapter_page_table: int32 [8], replicated, may hold values from 0 to 7, each once
Outputs:
- projected: bfloat16 [3072, 8192], P('rep', 'tp'), parts along dimension 0
There are 4 independent parts, one for each index of `rep`. A program takes and returns all parts, laid end to end along the dimension named above; an argument that names none is the same for every part. Nothing has to cross between parts.
Inputs may be any that keep to these rules, and one draw needn't show every extreme that they name: adapter_page_table is a permutation; adapter a is stored on tp device adapter_page_table[a] (each device holds exactly one adapter), and row adapter_page_table[a] of adapter_down_weight and adapter_up_weight holds it. `block_adapter_index`: the adapter used by all 128 tokens of a block.
All inputs are finite; a program needn't handle non-finite values.
Results may differ from a plain program's by a relative error of at most 0.0046.
Values may be sent and summed in bfloat16 or wider, within the bound.
A program may use at most 64 MiB of HBM per device.

v0:
```python
import jax
import jax.numpy as jnp
from jax import lax
from jax.sharding import PartitionSpec as P

adapter_scale = 2.0


def shards(
    attn,
    output_weight,
    adapter_down_weight,
    adapter_up_weight,
    block_adapter_index,
    adapter_page_table,
):
    tokens = attn.shape[0]
    blocks = block_adapter_index.shape[0]
    block_rows = tokens // blocks
    page_slot_count = adapter_down_weight.shape[0]
    pool_size = adapter_page_table.shape[0]
    width_out = output_weight.shape[1]
    position = lax.axis_index("tp")
    matches = block_adapter_index[:, None] == jnp.arange(pool_size, dtype=jnp.int32)[None, :]
    block_page_index = jnp.sum(jnp.where(matches, adapter_page_table[None, :], 0), axis=1)
    up_weight_columns = lax.all_to_all(
        adapter_up_weight, "tp", split_axis=2, concat_axis=0, tiled=True
    )
    block_up = up_weight_columns[block_page_index]
    shard_piece = lax.all_gather(attn, "tp", axis=1, tiled=True)
    base_output = jnp.dot(shard_piece, output_weight, preferred_element_type=jnp.float32)
    row_blocks = shard_piece.reshape(blocks, block_rows, shard_piece.shape[1])
    base_output, side_sum = (
        base_output,
        jnp.einsum(
            "btf,srf->bsrt", row_blocks, adapter_down_weight, preferred_element_type=jnp.float32
        ),
    )
    own_pages = position * page_slot_count + jnp.arange(page_slot_count, dtype=jnp.int32)
    owned = (block_page_index[:, None] == own_pages[None, :]).astype(jnp.float32)
    local_term = jnp.sum(owned[:, :, None, None] * side_sum, axis=1)
    shrunk = lax.psum(local_term.astype(jnp.bfloat16), "tp")
    adapter_output = jnp.einsum(
        "brt,brc->btc", shrunk, block_up, preferred_element_type=jnp.float32
    )
    adapter_output = adapter_output.reshape(tokens, width_out)
    return (base_output + adapter_scale * adapter_output).astype(jnp.bfloat16)


def solution(mesh):
    return jax.shard_map(
        shards,
        mesh=mesh,
        in_specs=(
            P("rep", "tp"),
            P(None, "tp"),
            P("tp", None, None),
            P("tp", None, None),
            P("rep"),
            P(),
        ),
        out_specs=P("rep", "tp"),
        check_vma=False,
    )
```

profile of v0, /device:TPU:0, one launch (start us, length us, event | category | flops | bytes accessed | tf_op | source)
XLA Modules:
  0.0 150.3 jit_solution(16534256131757500711)
XLA Ops:
  6.5 0.0 copy-start
  6.5 0.0 all-gather.2.cloned.1.call-start
  6.5 0.7 all-gather.2.cloned.1.call-update
  7.3 9.2 %copy.11 = bf16[1,64,8192]{1,0,2:T(2,128)(2,1)} copy(bf16[1,64,8192]{2,1,0:T(8,128)(2,1)} %param.9) | data formatting | bytes 2097152 | tf_op args[3]
  16.4 0.5 broadcast.42
  16.9 45.3 %reduce = bf16[8192,64]{1,0:T(8,128)(2,1)S(1)} reduce(bf16[8192,1,64]{2,1,0:T(2,128)(2,1)} %bitcast.36, bf16[]{:T(256)} %broadcast.42), dimensions={1}, to_apply=%bitcast.29.reduce_sub_computation | reduce | bytes 2097154
  62.2 0.0 copy-start.1
  62.2 0.0 copy-start.2
  62.2 2.7 %reshape.51 = bf16[8,2,32768]{2,1,0:T(2,128)(2,1)} reshape(bf16[8192,64]{1,0:T(8,128)(2,1)S(1)} %reduce) | data formatting | bytes 2097152
  64.9 5.2 %all-to-all-start = ((bf16[8,2,32768]{2,1,0:T(2,128)(2,1)}), bf16[8,2,32768]{2,1,0:T(2,128)(2,1)S(1)}, u32[]{:S(2)}, u32[]{:S(2)}) async-start(bf16[8,2,32768]{2,1,0:T(2,128)(2,1)} %reshape.51), calls=%async_computation | async-start | bytes 2097152 | tf_op jit(solution)/shard_map/all_to_all | solution.py:26
  70.1 0.2 all-reduce.2.cloned.1.call-start
  70.3 0.0 copy-done.1
  70.3 0.0 copy-done.2
  70.4 0.2 select_reduce_fusion
  70.6 0.0 all-gather.2.cloned.1.call-done
  70.6 0.0 copy-done
  70.6 5.5 %fusion.3 = bf16[6,64,128]{2,1,0:T(8,128)(2,1)} fusion(bf16[6,128,4096]{2,1,0:T(8,128)(2,1)} %bitcast.39, bf16[1,64,4096]{2,1,0:T(8,128)(2,1)S(1)} %copy-done, f32[6]{0:T(128)S(1)} %compare_convert_fusion), kind=kOutput, calls=%fused_computation.7 | convolution fusion | flops 402751488 | bytes 6914072 | tf_op jit(solution)/shard_map/btf,srf->bsrt/dot_general | solution.py:35
  76.0 0.0 all-reduce.2.cloned.1.call-update
  76.1 9.4 %all-to-all-done = bf16[8,2,32768]{2,1,0:T(2,128)(2,1)S(1)} async-done(((bf16[8,2,32768]{2,1,0:T(2,128)(2,1)}), bf16[8,2,32768]{2,1,0:T(2,128)(2,1)S(1)}, u32[]{:S(2)}, u32[]{:S(2)}) %all-to-all-start) | async-done | bytes 1048608 | tf_op jit(solution)/shard_map/all_to_all | solution.py:26
  85.5 4.3 %reshape.52 = bf16[8192,1,64]{2,1,0:T(2,128)(2,1)} reshape(bf16[8,2,32768]{2,1,0:T(2,128)(2,1)S(1)} %all-to-all-done) | data formatting | bytes 2097152
  89.9 2.5 %copy.16 = bf16[1,64,8192]{1,2,0:T(8,128)(2,1)S(1)} copy(bf16[1,64,8192]{1,0,2:T(2,128)(2,1)} %bitcast.37) | data formatting | bytes 2097152
  92.3 1.6 %copy.13 = bf16[1,64,8,1024]{3,1,2,0:T(8,128)(2,1)} copy(bf16[1,64,8,1024]{1,3,2,0:T(8,128)(2,1)S(1)} %bitcast.38) | data formatting | bytes 2097152 | tf_op jit(solution)/shard_map/all_to_all | solution.py:26
  93.9 1.8 %gather_fusion = bf16[6,64,1024]{2,1,0:T(8,128)(2,1)S(1)} fusion(bf16[8,64,1024]{2,1,0:T(8,128)(2,1)} %bitcast.40, s32[1024]{0:T(1024)S(1)} %pad_clamp_fusion), kind=kCustom, calls=%fused_computation | custom fusion | bytes 1572888 | tf_op jit(solution)/shard_map/gather | solution.py:29
  95.8 34.1 %all-reduce.2.cloned.1.call-done = bf16[6,64,128]{2,1,0:T(8,128)(2,1)} async-done(((bf16[6,64,128]{2,1,0:T(8,128)(2,1)}), bf16[6,64,128]{2,1,0:T(8,128)(2,1)}) %all-reduce.2.cloned.1.call-update) | async-done | bytes 98320 | tf_op jit(solution)/shard_map/psum | solution.py:42
  129.9 1.5 %convolution_multiply_fusion = f32[6,128,1024]{2,1,0:T(8,128)S(1)} fusion(bf16[6,64,128]{2,1,0:T(8,128)(2,1)} %all-reduce.2.cloned.1.call-done, bf16[6,64,1024]{2,1,0:T(8,128)(2,1)S(1)} %gather_fusion), kind=kOutput, calls=%fused_computation.3 | convolution fusion | flops 101449728 | bytes 4030464 | tf_op jit(solution)/shard_map/brt,brc->btc/dot_general | solution.py:43
  131.4 12.1 %fusion = bf16[768,1024]{1,0:T(8,128)(2,1)} fusion(f32[6,128,1024]{2,1,0:T(8,128)S(1)} %convolution_multiply_fusion, bf16[768,4096]{1,0:T(8,128)(2,1)} %all-gather.2.cloned.1.call-done, bf16[4096,1024]{1,0:T(8,128)(2,1)} %param.7), kind=kOutput, calls=%fused_computation.2 | convolution fusion | flops 6444023808 | bytes 19398656 | tf_op jit(solution)/shard_map/dot_general | solution.py:31
  (3 shorter events, 0.0 us)
Async XLA Ops:
  6.5 64.1 %copy-start = (bf16[1,64,4096]{2,1,0:T(8,128)(2,1)S(1)}, bf16[1,64,4096]{2,1,0:T(8,128)(2,1)}, u32[]{:S(2)}) copy-start(bf16[1,64,4096]{2,1,0:T(8,128)(2,1)} %param.8) | copy-start | bytes 1572868
  6.5 64.0 %all-gather.2.cloned.1.call-start = ((), (), s32[]{:S(2)}) async-start(), calls=%async_computation.1 | async-start | bytes 7077888 | tf_op jit(solution)/shard_map/all_gather | solution.py:30
  62.2 8.1 %copy-start.1 = (s32[8]{0:T(128)S(1)}, s32[8]{0:T(128)}, u32[]{:S(2)}) copy-start(s32[8]{0:T(128)} %param.11) | copy-start | bytes 100
  62.2 8.1 %copy-start.2 = (s32[6]{0:T(128)S(1)}, s32[6]{0:T(128)}, u32[]{:S(2)}) copy-start(s32[6]{0:T(128)} %param.10) | copy-start | bytes 76
  64.9 20.6 %all-to-all-start = ((bf16[8,2,32768]{2,1,0:T(2,128)(2,1)}), bf16[8,2,32768]{2,1,0:T(2,128)(2,1)S(1)}, u32[]{:S(2)}, u32[]{:S(2)}) async-start(bf16[8,2,32768]{2,1,0:T(2,128)(2,1)} %reshape.51), calls=%async_computation | async-start | bytes 2097152 | tf_op jit(solution)/shard_map/all_to_all | solution.py:26
  70.1 59.7 %all-reduce.2.cloned.1.call-start = ((), (), s32[]{:S(2)}) async-start(), calls=%async_computation.2 | async-start | bytes 196608 | tf_op jit(solution)/shard_map/psum | solution.py:42
Sparse Core Ops, SparseCore 0:
  9.2 49.2 all-gather.1
  76.2 53.6 all-reduce.1
where the time goes:
time: 151 us; the launch traced here: 150 us
  other arithmetic  45.5 us (30%)
  waiting for transfers between devices  44.3 us (29%)
  local copies, waits for them, and re-layouts  22.6 us (15%)
  matrix products  19.1 us (13%)
  between operations  13.5 us (9%)
  starting transfers between devices  5.45 us (4%)
    unnamed x1, other arithmetic  45.3 us
    psum x1, waiting for transfers between devices, shards(): shrunk = lax.psum(local_term.astype(jnp.bfloat16), 'tp')  34.1 us
    unnamed x11, local copies, waits for them, and re-layouts  19.2 us
    dot_general x1, matrix products, shards(): jnp.dot(shard_piece, output_weight, preferred_element_type=jnp.float32)  12.1 us
    all_to_all x1, waiting for transfers between devices, shards(): lax.all_to_all(adapter_up_weight, 'tp', split_axis=2, concat_axis=0, tile...  9.44 us
    dot_general x1, matrix products, shards(): jnp.einsum('btf,srf->bsrt', row_blocks, adapter_down_weight, preferred_el...  5.45 us
    all_to_all x1, starting transfers between devices, shards(): lax.all_to_all(adapter_up_weight, 'tp', split_axis=2, concat_axis=0, tile...  5.23 us
  transfers between devices with their start and end apart: 3, of which 2 were waited for; matrix products, arithmetic and copies ran while one was open for 49% of the time, Pallas kernels for 0%

commit v1 on v0

--- a/solution.py
+++ b/solution.py
@@ -39,7 +39,7 @@
     own_pages = position * page_slot_count + jnp.arange(page_slot_count, dtype=jnp.int32)
     owned = (block_page_index[:, None] == own_pages[None, :]).astype(jnp.float32)
     local_term = jnp.sum(owned[:, :, None, None] * side_sum, axis=1)
-    shrunk = lax.psum(local_term.astype(jnp.bfloat16), "tp")
+    shrunk = jnp.sum(lax.all_gather(local_term.astype(jnp.bfloat16), "tp"), axis=0)
     adapter_output = jnp.einsum(
         "brt,brc->btc", shrunk, block_up, preferred_element_type=jnp.float32
     )

time: 151 us -> 129 us (0.85)
  waiting for transfers between devices: 44.3 us -> 15.9 us
  blocking collectives: 0 us -> 9.62 us
  matrix products: 19.1 us -> 15.5 us
    psum x1 -> x0, waiting for transfers between devices: 34.1 us -> none  [shards(): shrunk = lax.psum(local_term.astype(jnp.bfloat16), 'tp')]
    all_gather x0 -> x1, blocking collectives: none -> 9.62 us  [shards(): lax.all_gather(local_term.astype(jnp.bfloat16), 'tp')]
    all_to_all x1, waiting for transfers between devices: 9.44 us -> 15.1 us  [shards(): lax.all_to_all(adapter_up_weight, 'tp', split_axis=2, concat_axis=0, tile...]
    dot_general x1, matrix products: 12.1 us -> 9.92 us  [shards(): jnp.dot(shard_piece, output_weight, preferred_element_type=jnp.float32)]
    unnamed x11 -> x15, local copies, waits for them, and re-layouts: 19.2 us -> 19.2 us
    unnamed x1 -> x2, other arithmetic: 45.3 us -> 45.3 us
  transfers between devices with their start and end apart: 3 -> 2, of which waited for: 2 -> 1; matrix products, arithmetic and copies ran while one was open for 49% -> 53% of each run, Pallas kernels for 0% -> 0%
where the time goes in v1:
time: 129 us; the launch traced here: 128 us
  other arithmetic  45.6 us (35%)
  local copies, waits for them, and re-layouts  22.6 us (18%)
  waiting for transfers between devices  15.9 us (12%)
  matrix products  15.5 us (12%)
  between operations  13.5 us (10%)
  blocking collectives  9.62 us (7%)
  starting transfers between devices  5.22 us (4%)
    unnamed x2, other arithmetic  45.3 us
    unnamed x15, local copies, waits for them, and re-layouts  19.2 us
    all_to_all x1, waiting for transfers between devices, shards(): lax.all_to_all(adapter_up_weight, 'tp', split_axis=2, concat_axis=0, tile...  15.1 us
    dot_general x1, matrix products, shards(): jnp.dot(shard_piece, output_weight, preferred_element_type=jnp.float32)  9.92 us
    all_gather x1, blocking collectives, shards(): lax.all_gather(local_term.astype(jnp.bfloat16), 'tp')  9.62 us
    all_to_all x1, starting transfers between devices, shards(): lax.all_to_all(adapter_up_weight, 'tp', split_axis=2, concat_axis=0, tile...  5.22 us
    dot_general x1, matrix products, shards(): jnp.einsum('btf,srf->bsrt', row_blocks, adapter_down_weight, preferred_el...  4.96 us
  transfers between devices with their start and end apart: 2, of which 1 were waited for; matrix products, arithmetic and copies ran while one was open for 53% of the time, Pallas kernels for 0%

profile of v1, /device:TPU:0, one launch (start us, length us, event | category | flops | bytes accessed | tf_op | source)
XLA Modules:
  0.0 127.9 jit_solution(10916704434097761115)
XLA Ops:
  6.5 0.0 copy-start
  6.5 0.0 all-gather.3.cloned.1.call-start
  6.5 0.7 all-gather.3.cloned.1.call-update
  7.3 9.2 %copy.13 = bf16[1,64,8192]{1,0,2:T(2,128)(2,1)} copy(bf16[1,64,8192]{2,1,0:T(8,128)(2,1)} %param.9) | data formatting | bytes 2097152 | tf_op args[3]
  16.4 0.5 broadcast.42
  17.0 45.3 %reduce.1 = bf16[8192,64]{1,0:T(8,128)(2,1)S(1)} reduce(bf16[8192,1,64]{2,1,0:T(2,128)(2,1)} %bitcast.39, bf16[]{:T(256)} %broadcast.42), dimensions={1}, to_apply=%bitcast.31.reduce_sub_computation | reduce | bytes 2097154
  62.2 0.0 copy-start.1
  62.2 0.0 copy-start.2
  62.2 2.7 %reshape.62 = bf16[8,2,32768]{2,1,0:T(2,128)(2,1)} reshape(bf16[8192,64]{1,0:T(8,128)(2,1)S(1)} %reduce.1) | data formatting | bytes 2097152
  64.9 5.2 %all-to-all-start = ((bf16[8,2,32768]{2,1,0:T(2,128)(2,1)}), bf16[8,2,32768]{2,1,0:T(2,128)(2,1)S(1)}, u32[]{:S(2)}, u32[]{:S(2)}) async-start(bf16[8,2,32768]{2,1,0:T(2,128)(2,1)} %reshape.62), calls=%async_computation | async-start | bytes 2097152 | tf_op jit(solution)/shard_map/all_to_all | solution.py:26
  70.1 0.0 copy-done.1
  70.1 0.0 copy-done.2
  70.1 0.2 select_reduce_fusion
  70.3 15.1 %all-to-all-done = bf16[8,2,32768]{2,1,0:T(2,128)(2,1)S(1)} async-done(((bf16[8,2,32768]{2,1,0:T(2,128)(2,1)}), bf16[8,2,32768]{2,1,0:T(2,128)(2,1)S(1)}, u32[]{:S(2)}, u32[]{:S(2)}) %all-to-all-start) | async-done | bytes 1048608 | tf_op jit(solution)/shard_map/all_to_all | solution.py:26
  85.5 4.3 %reshape.63 = bf16[8192,1,64]{2,1,0:T(2,128)(2,1)} reshape(bf16[8,2,32768]{2,1,0:T(2,128)(2,1)S(1)} %all-to-all-done) | data formatting | bytes 2097152
  89.8 2.5 %copy.18 = bf16[1,64,8192]{1,2,0:T(8,128)(2,1)S(1)} copy(bf16[1,64,8192]{1,0,2:T(2,128)(2,1)} %bitcast.40) | data formatting | bytes 2097152
  92.3 1.6 %copy.15 = bf16[1,64,8,1024]{3,1,2,0:T(8,128)(2,1)} copy(bf16[1,64,8,1024]{1,3,2,0:T(8,128)(2,1)S(1)} %bitcast.41) | data formatting | bytes 2097152 | tf_op jit(solution)/shard_map/all_to_all | solution.py:26
  93.9 1.8 %gather_fusion = bf16[6,64,1024]{2,1,0:T(8,128)(2,1)S(1)} fusion(bf16[8,64,1024]{2,1,0:T(8,128)(2,1)} %bitcast.45, s32[1024]{0:T(1024)S(1)} %pad_clamp_fusion), kind=kCustom, calls=%fused_computation | custom fusion | bytes 1572888 | tf_op jit(solution)/shard_map/gather | solution.py:29
  95.7 0.0 all-gather.3.cloned.1.call-done
  95.8 0.0 slice-start
  95.8 0.0 copy-done
  95.8 0.0 slice-start.1
  95.8 5.0 %fusion.3 = bf16[6,1,64,128]{3,2,1,0:T(8,128)(2,1)S(1)} fusion(bf16[6,128,4096]{2,1,0:T(8,128)(2,1)} %bitcast.42, bf16[1,64,4096]{2,1,0:T(8,128)(2,1)S(1)} %copy-done, f32[6]{0:T(128)S(1)} %compare_convert_fusion), kind=kOutput, calls=%fused_computation.7 | convolution fusion | flops 402751488 | bytes 6914072 | tf_op jit(solution)/shard_map/btf,srf->bsrt/dot_general | solution.py:35
  100.8 9.6 %all-gather = bf16[48,1,64,128]{3,2,1,0:T(8,128)(2,1)S(1)} all-gather(bf16[6,1,64,128]{3,2,1,0:T(8,128)(2,1)S(1)} %fusion.3), channel_id=2, replica_groups=mesh['rep'=4,'tp'=8] {'tp'}, dimensions={0}, use_global_device_ids=true | all-gather | bytes 884736 | tf_op jit(solution)/shard_map/all_gather | solution.py:42
  110.4 0.1 bitcast_reduce_fusion
  110.5 0.6 convolution_multiply_fusion
  111.1 0.0 slice-done
  111.1 0.0 slice-done.1
  111.2 9.9 %fusion = bf16[768,1024]{1,0:T(8,128)(2,1)} fusion(f32[6,128,1024]{2,1,0:T(8,128)S(1)} %convolution_multiply_fusion, bf16[768,4096]{1,0:T(8,128)(2,1)S(1)} %bitcast.44, bf16[4096,1024]{1,0:T(8,128)(2,1)} %param.7), kind=kOutput, calls=%fused_computation.2 | convolution fusion | flops 6444023808 | bytes 19398656 | tf_op jit(solution)/shard_map/dot_general | solution.py:31
  (4 shorter events, 0.0 us)
Async XLA Ops:
  6.5 89.3 %copy-start = (bf16[1,64,4096]{2,1,0:T(8,128)(2,1)S(1)}, bf16[1,64,4096]{2,1,0:T(8,128)(2,1)}, u32[]{:S(2)}) copy-start(bf16[1,64,4096]{2,1,0:T(8,128)(2,1)} %param.8) | copy-start | bytes 1572868
  6.5 89.2 %all-gather.3.cloned.1.call-start = ((), (), s32[]{:S(2)}) async-start(), calls=%async_computation.1 | async-start | bytes 7077888 | tf_op jit(solution)/shard_map/all_gather | solution.py:30
  62.2 7.9 %copy-start.1 = (s32[8]{0:T(128)S(1)}, s32[8]{0:T(128)}, u32[]{:S(2)}) copy-start(s32[8]{0:T(128)} %param.11) | copy-start | bytes 100
  62.2 7.9 %copy-start.2 = (s32[6]{0:T(128)S(1)}, s32[6]{0:T(128)}, u32[]{:S(2)}) copy-start(s32[6]{0:T(128)} %param.10) | copy-start | bytes 76
  64.9 20.6 %all-to-all-start = ((bf16[8,2,32768]{2,1,0:T(2,128)(2,1)}), bf16[8,2,32768]{2,1,0:T(2,128)(2,1)S(1)}, u32[]{:S(2)}, u32[]{:S(2)}) async-start(bf16[8,2,32768]{2,1,0:T(2,128)(2,1)} %reshape.62), calls=%async_computation | async-start | bytes 2097152 | tf_op jit(solution)/shard_map/all_to_all | solution.py:26
  95.8 15.4 %slice-start = ((s8[6291456]{0:T(1024)(128)(4,1)}), s8[4194304]{0:T(1024)(128)(4,1)S(1)}, s32[]{:S(2)}) async-start(s8[6291456]{0:T(1024)(128)(4,1)} %bitcast.43), calls=%async_computation.2 | async-start | bytes 8388608
  95.8 15.3 %slice-start.1 = ((s8[6291456]{0:T(1024)(128)(4,1)}), s8[2097152]{0:T(1024)(128)(4,1)S(1)}, s32[]{:S(2)}) async-start(s8[6291456]{0:T(1024)(128)(4,1)} %bitcast.43), calls=%async_computation.3 | async-start | bytes 4194304
Sparse Core Ops, SparseCore 0:
  9.2 49.2 all-gather.2
